TPU v7x, 256 devices: a whole 4x4x8 slice. The times are simulated.
256 devices in a mesh: ulysses: 16 (over z, x_hi), blk: 16 (over y, x_lo, core).
Axes of the slice: x: 4 (x_hi: 2, x_lo: 2; x = x_hi * 2 + x_lo), y: 4, z: 8, core: 2. Of those that a mesh axis runs over, the one named last changes fastest.
Arguments:
- queries: bfloat16 [16, 1024, 4096], P('blk', 'ulysses'), may hold values from -6 to 6
- key_rows: bfloat16 [16, 1024, 1024], P('blk', 'ulysses'), may hold values from -6 to 6
- value_rows: bfloat16 [16, 1024, 1024], P('blk', 'ulysses'), may hold values from -6 to 6
- tile_segment: int32 [128], replicated, may hold values from 0 to 31, never falling along the last dimension, each value on 1 to 8 neighbouring positions
Outputs:
- attended: bfloat16 [16, 1024, 4096], P('blk', 'ulysses')
Inputs may be any that keep to these rules, and one draw needn't show every extreme that they name: `tile_segment`: segment numbers never fall along the sequence and each segment covers 1 to 8 tiles.
All inputs are finite; a program needn't handle non-finite values.
Results may differ from a plain program's by a relative error of at most 0.0045.
Values may be sent and summed in bfloat16 or wider, within the bound.
A program may use at most 64 MiB of HBM per device.

v0:
```python
import math

import jax
import jax.numpy as jnp
from jax import lax
from jax.sharding import PartitionSpec as P

HEAD_DIM = 128
TILE = 128


masked_score = -1e30


def side_by_side(arrays, axis, split_dim, concat_dim, along):
    widths = [a.shape[along] for a in arrays]
    both = jnp.concatenate(arrays, axis=along)
    whole = lax.all_to_all(both, axis, split_axis=split_dim, concat_axis=concat_dim, tiled=True)
    return tuple(jnp.split(whole, [sum(widths[:k]) for k in range(1, len(widths))], axis=along))


def partner_2(value, axis, bit):
    return lax.ppermute(value, axis, [(i, i ^ 1 << bit) for i in range(lax.axis_size(axis))])


def side_by_side_2(arrays, axis, dim, along):
    ends, at = ([], 0)
    for a in arrays[:-1]:
        at += a.shape[along]
        ends.append(at)
    both = jnp.concatenate(arrays, axis=along)
    return tuple(jnp.split(lax.all_gather(both, axis, axis=dim, tiled=True), ends, axis=along))


def segment_of(positions, tile_segment):
    tiles_total = tile_segment.shape[0]
    matches = (positions // TILE)[:, None] == jnp.arange(tiles_total, dtype=jnp.int32)[None, :]
    return jnp.sum(jnp.where(matches, tile_segment[None, :], 0), axis=1)


def visible(query_pos, query_seg, key_pos, key_seg):
    earlier = key_pos[None, :] <= query_pos[:, None]
    same_image = (key_seg[None, :] == query_seg[:, None]) & (query_seg[:, None] % 2 == 1)
    return earlier | same_image


def widen(source_rows, groups):
    tokens_dev = source_rows.shape[1]
    heads_here = source_rows.shape[2] // HEAD_DIM
    factor = max(1, groups // heads_here)
    spread = jnp.repeat(source_rows.reshape(1, tokens_dev, heads_here, HEAD_DIM), factor, axis=2)
    return spread.reshape(1, tokens_dev, heads_here * factor * HEAD_DIM)


def same_rows(row_ids):
    return row_ids


def update(current, allowed, query_block, key_block, value_block):
    maxima, denominators, weighted = current
    scores = jnp.einsum(
        "qkgd,skd->kgqs", query_block, key_block, preferred_element_type=jnp.float32
    )
    scores = jnp.where(allowed[None, None], scores * HEAD_DIM ** (-0.5), masked_score)
    new_max = jnp.maximum(maxima, jnp.max(scores, axis=3))
    weights = jnp.where(allowed[None, None], jnp.exp(scores - new_max[..., None]), 0.0)
    factor = jnp.exp(maxima - new_max)
    denominators = factor * denominators + jnp.sum(weights, axis=3)
    product = jnp.einsum(
        "kgqs,skd->kgqd",
        weights.astype(jnp.bfloat16),
        value_block,
        preferred_element_type=jnp.float32,
    )
    weighted = factor[..., None] * weighted + product
    return (new_max, denominators, weighted)


def keep_state(current, allowed, query_block, key_block, value_block):
    return current


def build_fold(query_rows, query_pos, tile_segment, key_position, kv_width):
    rows_total = query_rows.shape[0]
    kv_local = kv_width // HEAD_DIM
    group_size = query_rows.shape[1] // HEAD_DIM // kv_local
    shaped = query_rows.reshape(rows_total, kv_local, group_size, HEAD_DIM)
    query_seg = segment_of(query_pos, tile_segment)
    half_rows = rows_total // 2

    def fold_step(running, portion, offset):
        key_part, value_part = portion
        portion_rows = key_part.shape[0]
        block_rows = math.gcd(portion_rows, 512)
        block_total = portion_rows // block_rows
        key_blocks = key_part.reshape(block_total, block_rows, kv_local, HEAD_DIM)
        value_blocks = value_part.reshape(block_total, block_rows, kv_local, HEAD_DIM)

        def one_block(halves, inputs):
            key_block, value_block, block_number = inputs
            key_pos = key_position(
                block_number * block_rows + jnp.arange(block_rows, dtype=jnp.int32)
            )
            key_seg = segment_of(key_pos, tile_segment)
            results = []
            for half_index in range(2):
                row_low = half_index * half_rows
                row_high = row_low + half_rows
                allowed = visible(
                    query_pos[row_low:row_high], query_seg[row_low:row_high], key_pos, key_seg
                )
                results.append(
                    lax.cond(
                        jnp.any(allowed),
                        update,
                        keep_state,
                        halves[half_index],
                        allowed,
                        shaped[row_low:row_high],
                        key_block,
                        value_block,
                    )
                )
            return ((results[0], results[1]), None)

        running, unused = lax.scan(
            one_block, running, (key_blocks, value_blocks, jnp.arange(block_total, dtype=jnp.int32))
        )
        return running

    def empty_half():
        return (
            jnp.full((kv_local, group_size, half_rows), masked_score, jnp.float32),
            jnp.zeros((kv_local, group_size, half_rows), jnp.float32),
            jnp.zeros((kv_local, group_size, half_rows, HEAD_DIM), jnp.float32),
        )

    return (fold_step, (empty_half(), empty_half()))


def finish(running):
    outputs = [weighted / denominators[..., None] for maxima, denominators, weighted in running]
    joined = jnp.concatenate(outputs, axis=2)
    kv_local, group_size, rows_total, head_dim = joined.shape
    joined = jnp.transpose(joined, (2, 0, 1, 3)).reshape(
        rows_total, kv_local * group_size * head_dim
    )
    return joined.astype(jnp.bfloat16)


def local(queries, key_rows, value_rows, tile_segment):
    ulysses_count = lax.axis_size("ulysses")
    block_count = lax.axis_size("blk")
    tokens_dev = queries.shape[1]
    block_len = tokens_dev * ulysses_count
    block_index = lax.axis_index("blk")
    local_rows = jnp.arange(block_len, dtype=jnp.int32)
    moved = (
        lax.all_to_all(queries, "ulysses", split_axis=2, concat_axis=1, tiled=True),
        *side_by_side(
            (widen(key_rows, ulysses_count), widen(value_rows, ulysses_count)), "ulysses", 2, 1, 0
        ),
    )
    query_rows, key_local, value_local = (moved[0][0], moved[1][0], moved[2][0])
    half_rows = block_len // 2
    partner = block_count - 1 - block_index
    travelling = query_rows[half_rows:]
    for bit_index in range(block_count.bit_length() - 1):
        travelling = partner_2(travelling, "blk", bit_index)
    query_rows = jnp.concatenate([query_rows[:half_rows], travelling], axis=0)
    query_pos = jnp.concatenate(
        [
            block_index * block_len + local_rows[:half_rows],
            partner * block_len + local_rows[half_rows:],
        ]
    )
    fold_step, initial = build_fold(
        query_rows, query_pos, tile_segment, same_rows, key_local.shape[1]
    )
    running = fold_step(
        initial, side_by_side_2((key_local, value_local), "blk", 0, 1), jnp.int32(0)
    )
    out_rows = finish(running)
    returning = out_rows[half_rows:]
    for bit_index in range(block_count.bit_length() - 1):
        returning = partner_2(returning, "blk", bit_index)
    out_rows = jnp.concatenate([out_rows[:half_rows], returning], axis=0)
    attended = lax.all_to_all(out_rows[None], "ulysses", split_axis=1, concat_axis=2, tiled=True)
    return attended


def solution(mesh):
    return jax.shard_map(
        local,
        mesh=mesh,
        in_specs=(
            P("blk", "ulysses", None),
            P("blk", "ulysses", None),
            P("blk", "ulysses", None),
            P(),
        ),
        out_specs=P("blk", "ulysses", None),
        check_vma=False,
    )
```

profile of v0, /device:TPU:17, one launch (start us, length us, event | category | flops | bytes accessed | tf_op | source)
XLA Modules:
  0.0 424.8 jit_solution(16484188474409896511)
XLA Ops:
  10.6 27.8 %all_to_all.48 = bf16[16,2,8192]{2,1,0:T(2,128)(2,1)S(1)} all-to-all(bf16[16,2,8192]{2,1,0:T(2,128)(2,1)S(1)} %reshape.218), channel_id=1, replica_groups=mesh['ulysses'=16,'blk'=16] {'ulysses'}, dimensions={0} | all-to-all | bytes 1048576 | tf_op jit(solution)/shard_map/all_to_all | solution.py:18
  40.9 2.8 copy.75
  44.2 22.5 %reduce.4 = bf16[4096,64]{1,0:T(8,128)(2,1)S(1)} reduce(bf16[4096,1,64]{2,1,0:T(2,128)(2,1)S(1)} %bitcast.147, bf16[]{:T(256)} %broadcast.213), dimensions={1}, to_apply=%bitcast.127.reduce_sub_computation | reduce | bytes 1048578
  67.4 21.9 %all_to_all.49 = bf16[16,2,8192]{2,1,0:T(2,128)(2,1)S(1)} all-to-all(bf16[16,2,8192]{2,1,0:T(2,128)(2,1)S(1)} %reshape.220), channel_id=1, replica_groups=mesh['ulysses'=16,'blk'=16] {'ulysses'}, dimensions={0} | all-to-all | bytes 1048576 | tf_op jit(solution)/shard_map/all_to_all | solution.py:159
  90.5 2.3 copy.76
  93.1 2.8 collective-permute-start
  97.4 7.2 %collective-permute-done.1 = bf16[512,256]{1,0:T(8,128)(2,1)S(1)} collective-permute-done((bf16[512,256]{1,0:T(8,128)(2,1)S(1)}, bf16[512,256]{1,0:T(8,128)(2,1)S(1)}, u32[]{:S(2)}, u32[]{:S(2)}) %collective-permute-start.1) | collective-permute-done | bytes 262176 | tf_op jit(solution)/shard_map/ppermute | solution.py:23
  105.7 5.5 %collective-permute-done.2 = bf16[512,256]{1,0:T(8,128)(2,1)S(1)} collective-permute-done((bf16[512,256]{1,0:T(8,128)(2,1)S(1)}, bf16[512,256]{1,0:T(8,128)(2,1)S(1)}, u32[]{:S(2)}, u32[]{:S(2)}) %collective-permute-start.2) | collective-permute-done | bytes 262176 | tf_op jit(solution)/shard_map/ppermute | solution.py:23
  111.8 6.7 %collective-permute-done.3 = bf16[512,256]{1,0:T(8,128)(2,1)S(1)} collective-permute-done((bf16[512,256]{1,0:T(8,128)(2,1)S(1)}, bf16[512,256]{1,0:T(8,128)(2,1)S(1)}, u32[]{:S(2)}, u32[]{:S(2)}) %collective-permute-start.3) | collective-permute-done | bytes 262176 | tf_op jit(solution)/shard_map/ppermute | solution.py:23
  119.6 5.7 %fusion.52 = (bf16[16384,128]{1,0:T(8,128)(2,1)}, bf16[16384,128]{1,0:T(8,128)(2,1)}) fusion(bf16[16384,256]{1,0:T(8,128)(2,1)} %all-gather.2.cloned.1.call-done), kind=kLoop, calls=%fused_computation.100 | loop fusion | bytes 16777216 | tf_op jit(solution)/shard_map/split | solution.py:32
  125.4 234.0 %while.23 = (s32[]{:T(128)}, f32[1,2,512]{2,1,0:T(2,128)S(1)}, f32[1,2,512]{2,1,0:T(2,128)S(1)}, f32[1,2,512,128]{3,2,1,0:T(8,128)S(1)}, f32[1,2,512]{2,1,0:T(2,...) while((s32[]{:T(128)}, f32[1,2,512]{2,1,0:T(2,128)S(1)}, ...), condition=%wide.region_13.14_spmd, body=%wide.region_1.13_spmd.sunk | while | flops 553869824 | bytes 18521024 | solution.py:126
  130.5 2.2 conditional.5
  132.7 2.2 conditional.4
  137.4 1.3 fusion.61
  139.9 2.2 conditional.5
  142.0 2.2 conditional.4
  146.7 1.3 fusion.61
  149.3 2.2 conditional.5
  151.4 2.2 conditional.4
  158.6 2.2 conditional.5
  160.8 2.2 conditional.4
  165.5 1.3 fusion.61
  168.0 2.2 conditional.5
  170.2 2.2 conditional.4
  174.9 1.3 fusion.61
  177.4 2.2 conditional.5
  179.6 2.2 conditional.4
  186.8 2.2 conditional.5
  188.9 2.2 conditional.4
  193.6 1.3 fusion.61
  196.2 2.2 conditional.5
  198.3 2.2 conditional.4
  205.5 2.2 conditional.5
  207.7 2.2 conditional.4
  212.4 1.3 fusion.61
  214.9 2.2 conditional.5
  217.1 2.2 conditional.4
  221.8 1.3 fusion.61
  224.3 2.2 conditional.5
  226.5 2.2 conditional.4
  233.7 2.2 conditional.5
  235.8 2.2 conditional.4
  240.5 1.3 fusion.61
  243.1 2.2 conditional.5
  245.2 2.2 conditional.4
  249.9 1.3 fusion.61
  252.4 2.2 conditional.5
  254.6 2.2 conditional.4
  261.9 2.2 conditional.4
  266.6 1.3 fusion.61
  269.1 2.2 conditional.4
  276.3 2.2 conditional.4
  281.0 1.3 fusion.61
  283.6 2.2 conditional.4
  288.3 1.3 fusion.61
  290.8 2.2 conditional.4
  295.5 1.3 fusion.61
  360.1 5.2 %collective-permute-start.4 = (bf16[512,256]{0,1:T(8,128)(2,1)S(1)}, bf16[512,256]{0,1:T(8,128)(2,1)S(1)}, u32[]{:S(2)}, u32[]{:S(2)}) collective-permute-start(bf16[512,256]{0,1:T(8,128)(2,1)S(1)} %bitcast.169), channel_id=1, source_target_pairs={{0,1},{1,0},{2,3},{3,2},{4,5},{5,4},{6,7},{7,6},{8,9},{9,8},{10,11... | collective-permute-start | bytes 786440 | tf_op jit(solution)/shard_map/ppermute | solution.py:23
  366.4 7.5 %collective-permute-done.5 = bf16[512,256]{0,1:T(8,128)(2,1)S(1)} collective-permute-done((bf16[512,256]{0,1:T(8,128)(2,1)S(1)}, bf16[512,256]{0,1:T(8,128)(2,1)S(1)}, u32[]{:S(2)}, u32[]{:S(2)}) %collective-permute-start.5) | collective-permute-done | bytes 262176 | tf_op jit(solution)/shard_map/ppermute | solution.py:23
  373.9 3.2 collective-permute-start.6
  377.1 5.5 %collective-permute-done.6 = bf16[512,256]{0,1:T(8,128)(2,1)S(1)} collective-permute-done((bf16[512,256]{0,1:T(8,128)(2,1)S(1)}, bf16[512,256]{0,1:T(8,128)(2,1)S(1)}, u32[]{:S(2)}, u32[]{:S(2)}) %collective-permute-start.6) | collective-permute-done | bytes 262176 | tf_op jit(solution)/shard_map/ppermute | solution.py:23
  382.7 7.4 %collective-permute-done.7 = bf16[512,256]{0,1:T(8,128)(2,1)S(1)} collective-permute-done((bf16[512,256]{0,1:T(8,128)(2,1)S(1)}, bf16[512,256]{0,1:T(8,128)(2,1)S(1)}, u32[]{:S(2)}, u32[]{:S(2)}) %collective-permute-start.7) | collective-permute-done | bytes 262176 | tf_op jit(solution)/shard_map/ppermute | solution.py:23
  391.1 3.9 reduce.5
  395.1 21.5 %all_to_all.50 = bf16[16,2,8192]{2,1,0:T(2,128)(2,1)S(1)} all-to-all(bf16[16,2,8192]{2,1,0:T(2,128)(2,1)S(1)} %reshape.222), channel_id=1, replica_groups=mesh['ulysses'=16,'blk'=16] {'ulysses'}, dimensions={0} | all-to-all | bytes 1048576 | tf_op jit(solution)/shard_map/all_to_all | solution.py:188
  (507 shorter events, 171.8 us)
Async XLA Ops:
  6.5 113.1 %all-gather.2.cloned.1.call-start = ((), (), s32[]{:S(2)}) async-start(), calls=%async_computation.3 | async-start | bytes 8912896 | tf_op jit(solution)/shard_map/all_gather | solution.py:32
  39.8 1.1 copy-start
  92.8 18.5 %copy-start.1 = (s32[128]{0:T(128)S(1)}, s32[128]{0:T(128)}, u32[]{:S(2)}) copy-start(s32[128]{0:T(128)} %param.13) | copy-start | bytes 1540
  93.1 4.0 collective-permute-start
  97.1 7.5 %collective-permute-start.1 = (bf16[512,256]{1,0:T(8,128)(2,1)S(1)}, bf16[512,256]{1,0:T(8,128)(2,1)S(1)}, u32[]{:S(2)}, u32[]{:S(2)}) collective-permute-start(bf16[512,256]{1,0:T(8,128)(2,1)S(1)} %collective-permute-done), channel_id=1, source_target_pairs={{0,2},{1,3},{2,0},{3,1},{4,6},{5,7},{6,4},{7,5},{8,10},{9,11},{10,... | collective-permute-start | bytes 786440 | tf_op jit(solution)/shard_map/ppermute | solution.py:23
  104.6 6.6 %collective-permute-start.2 = (bf16[512,256]{1,0:T(8,128)(2,1)S(1)}, bf16[512,256]{1,0:T(8,128)(2,1)S(1)}, u32[]{:S(2)}, u32[]{:S(2)}) collective-permute-start(bf16[512,256]{1,0:T(8,128)(2,1)S(1)} %collective-permute-done.1), channel_id=1, source_target_pairs={{0,4},{1,5},{2,6},{3,7},{4,0},{5,1},{6,2},{7,3},{8,12},{9,13},{10,... | collective-permute-start | bytes 786440 | tf_op jit(solution)/shard_map/ppermute | solution.py:23
  111.2 7.3 %collective-permute-start.3 = (bf16[512,256]{1,0:T(8,128)(2,1)S(1)}, bf16[512,256]{1,0:T(8,128)(2,1)S(1)}, u32[]{:S(2)}, u32[]{:S(2)}) collective-permute-start(bf16[512,256]{1,0:T(8,128)(2,1)S(1)} %collective-permute-done.2), channel_id=1, source_target_pairs={{0,8},{1,9},{2,10},{3,11},{4,12},{5,13},{6,14},{7,15},{8,0},{9,1},... | collective-permute-start | bytes 786440 | tf_op jit(solution)/shard_map/ppermute | solution.py:23
  360.1 6.3 %collective-permute-start.4 = (bf16[512,256]{0,1:T(8,128)(2,1)S(1)}, bf16[512,256]{0,1:T(8,128)(2,1)S(1)}, u32[]{:S(2)}, u32[]{:S(2)}) collective-permute-start(bf16[512,256]{0,1:T(8,128)(2,1)S(1)} %bitcast.169), channel_id=1, source_target_pairs={{0,1},{1,0},{2,3},{3,2},{4,5},{5,4},{6,7},{7,6},{8,9},{9,8},{10,11... | collective-permute-start | bytes 786440 | tf_op jit(solution)/shard_map/ppermute | solution.py:23
  366.4 7.5 %collective-permute-start.5 = (bf16[512,256]{0,1:T(8,128)(2,1)S(1)}, bf16[512,256]{0,1:T(8,128)(2,1)S(1)}, u32[]{:S(2)}, u32[]{:S(2)}) collective-permute-start(bf16[512,256]{0,1:T(8,128)(2,1)S(1)} %collective-permute-done.4), channel_id=1, source_target_pairs={{0,2},{1,3},{2,0},{3,1},{4,6},{5,7},{6,4},{7,5},{8,10},{9,11},{10,... | collective-permute-start | bytes 786440 | tf_op jit(solution)/shard_map/ppermute | solution.py:23
  373.9 8.7 %collective-permute-start.6 = (bf16[512,256]{0,1:T(8,128)(2,1)S(1)}, bf16[512,256]{0,1:T(8,128)(2,1)S(1)}, u32[]{:S(2)}, u32[]{:S(2)}) collective-permute-start(bf16[512,256]{0,1:T(8,128)(2,1)S(1)} %collective-permute-done.5), channel_id=1, source_target_pairs={{0,4},{1,5},{2,6},{3,7},{4,0},{5,1},{6,2},{7,3},{8,12},{9,13},{10,... | collective-permute-start | bytes 786440 | tf_op jit(solution)/shard_map/ppermute | solution.py:23
  382.6 7.6 %collective-permute-start.7 = (bf16[512,256]{0,1:T(8,128)(2,1)S(1)}, bf16[512,256]{0,1:T(8,128)(2,1)S(1)}, u32[]{:S(2)}, u32[]{:S(2)}) collective-permute-start(bf16[512,256]{0,1:T(8,128)(2,1)S(1)} %collective-permute-done.6), channel_id=1, source_target_pairs={{0,8},{1,9},{2,10},{3,11},{4,12},{5,13},{6,14},{7,15},{8,0},{9,1},... | collective-permute-start | bytes 786440 | tf_op jit(solution)/shard_map/ppermute | solution.py:23
Sparse Core Ops, SparseCore 0:
  41.0 55.6 all-gather.1
where the time goes:
time: 430 us; the launch traced here: 425 us
  other arithmetic  98.7 us (23%)
  local copies, waits for them, and re-layouts  73.2 us (17%)
  blocking collectives  71.1 us (17%)
  loops' own time  63.6 us (15%)
  matrix products  49.4 us (11%)
  waiting for transfers between devices  42.1 us (10%)
  between operations  13.8 us (3%)
  starting transfers between devices  12.9 us (3%)
    another operation x1, loops' own time, fold_step(): lax.scan(one_block, running, (key_blocks, value_blocks, jnp.arange(block_...  61.4 us
    ppermute x8, waiting for transfers between devices, partner_2(): lax.ppermute(value, axis, [(i, i ^ 1 << bit) for i in range(lax.axis_size...  42.1 us
    reduce_or x32, other arithmetic, one_block(): jnp.any(allowed)  41.9 us
    squeeze x32, local copies, waits for them, and re-layouts, fold_step(): lax.scan(one_block, running, (key_blocks, value_blocks, jnp.arange(block_...  31.8 us
    dot_general x33, matrix products, update(): jnp.einsum('kgqs,skd->kgqd', weights.astype(jnp.bfloat16), value_block, p...  31.2 us
    all_to_all x1, blocking collectives, side_by_side(): lax.all_to_all(both, axis, split_axis=split_dim, concat_axis=concat_dim,...  27.8 us
    unnamed x2, other arithmetic  26.3 us
    all_to_all x1, blocking collectives, local(): lax.all_to_all(queries, 'ulysses', split_axis=2, concat_axis=1, tiled=True)  21.9 us
  transfers between devices with their start and end apart: 9, of which 8 were waited for; matrix products, arithmetic and copies ran while one was open for 7% of the time, Pallas kernels for 0%

commit v1 on v0

v1 whole, which is shorter than its diff:
```python
import math

import jax
import jax.numpy as jnp
from jax import lax
from jax.experimental import pallas as pl
from jax.experimental.pallas import tpu as pltpu
from jax.sharding import PartitionSpec as P

MESH = pl.DeviceIdType.MESH
D = 128
SCALE = D**-0.5 * math.log2(math.e)
MASKED = -1e30
ROWS = 64
ROUNDS = (
    ((0, 0), (1, 0), (3, 0), (0, 1), (0, 3)),
    ((2, 0), (0, 2), (1, 1), (1, 3), (3, 1), (3, 3)),
    ((2, 1), (2, 3), (1, 2), (3, 2), (2, 2)),
)


def attend(q, k, v, mask, rows, m_ref, l_ref, acc_ref):
    s = lax.dot_general(q, k, (((1,), (1,)), ((), ())), preferred_element_type=jnp.float32)
    if mask is not None:
        s = jnp.where(mask, s, MASKED)
    m_old = m_ref[rows, :]
    peak = jnp.max(s, axis=1, keepdims=True) * SCALE
    m_new = jnp.maximum(m_old, jnp.broadcast_to(peak, m_old.shape))
    alpha = jnp.exp2(m_old - m_new)
    p = jnp.exp2(s * SCALE - m_new[:, :1]).astype(jnp.bfloat16)
    both = jnp.concatenate([v, jnp.ones_like(v)], axis=1)
    o = lax.dot_general(p, both, (((1,), (0,)), ((), ())), preferred_element_type=jnp.float32)
    acc_ref[rows, :] = acc_ref[rows, :] * alpha + o[:, :D]
    l_ref[rows, :] = l_ref[rows, :] * alpha + o[:, D:]
    m_ref[rows, :] = m_new


def kernel(
    seg_ref, q_hbm, k_hbm, v_hbm, out_hbm,
    kv, qd, od, m_ref, l_ref, acc_ref,
    kv_send, kv_recv, q_send, q_recv, g_send, g_recv, c_send, c_recv, o_send, o_recv, here,
):
    u = lax.axis_index("ulysses")
    b = lax.axis_index("blk")
    z, xh = u // 2, u % 2
    y, xl, c = b // 4, (b // 2) % 2, b % 2
    x = 2 * xh + xl
    mirror = 15 - b

    def chip(xx, yy):
        return (2 * z + xx // 2, 4 * yy + 2 * (xx % 2) + c)

    def copy(src, dst, send, recv, device):
        return pltpu.make_async_remote_copy(
            src_ref=src, dst_ref=dst, send_sem=send, recv_sem=recv, device_id=device, device_id_type=MESH
        )

    plane = [(z + d) % 8 for d in range(8)]
    back = [(z + 8 - d) % 8 for d in range(8)]
    xs = [(x + d) % 4 for d in range(4)]
    ys = [(y + d) % 4 for d in range(4)]
    partner = (u, b + 1 - 2 * c)

    barrier = pltpu.get_barrier_semaphore()
    peers = [(2 * plane[d] + xh, b) for d in range(1, 8)] + [(2 * plane[d] + xh, mirror) for d in range(8)]
    peers += [chip(xs[1], y), chip(xs[3], y), chip(x, ys[1]), chip(x, ys[3]), partner]
    for peer in peers:
        pl.semaphore_signal(barrier, inc=1, device_id=peer, device_id_type=MESH)
    pl.semaphore_wait(barrier, len(peers))

    waits = []

    def kv_group(group, t):
        return kv.at[b, xh, group // 4, t, pl.ds(pl.multiple_of((group % 4) * ROWS, ROWS), ROWS)]

    def columns(ref, start, width):
        return ref.at[:, pl.ds(pl.multiple_of(start, width), width)]

    locals_ = []
    for t, ref in enumerate((k_hbm, v_hbm)):
        own = pltpu.make_async_copy(columns(ref, z * D, D), kv_group(z, t), here.at[t])
        own.start()
        locals_.append(own)
    order = (4, 3, 5, 2, 6, 1, 7)
    for d in order:
        for t, ref in enumerate((k_hbm, v_hbm)):
            go = copy(
                columns(ref, plane[d] * D, D), kv_group(z, t), kv_send.at[t, d], kv_recv.at[t, d],
                (2 * plane[d] + xh, b),
            )
            go.start()
            waits.append(go)
    q_own = pltpu.make_async_copy(columns(q_hbm, z * 4 * D, 2 * D), qd.at[0, z], here.at[2])
    q_own.start()
    for d in order + (0,):
        for job in range(2):
            if job == 0 and d == 0:
                continue
            go = copy(
                columns(q_hbm, plane[d] * 4 * D + job * 2 * D, 2 * D), qd.at[job, z],
                q_send.at[job, d], q_recv.at[job, d], (2 * plane[d] + xh, mirror if job else b),
            )
            go.start()
            waits.append(go)

    m_ref[...] = jnp.full(m_ref.shape, MASKED, jnp.float32)
    l_ref[...] = jnp.zeros(l_ref.shape, jnp.float32)
    acc_ref[...] = jnp.zeros(acc_ref.shape, jnp.float32)

    for own in locals_:
        own.wait()
    for d in order:
        for t, ref in enumerate((k_hbm, v_hbm)):
            copy(
                columns(ref, z * D, D), kv_group(back[d], t), kv_send.at[t, d], kv_recv.at[t, d], (u, mirror)
            ).wait_recv()

    def unit(h, p, s, core):
        xx, yy = (xs[p], ys[s]) if h == 0 else (xs[s], ys[p])
        return kv.at[4 * yy + 2 * (xx % 2) + core, xx // 2, h]

    def neighbour(h, axis, step):
        along_x = (axis == 0) == (h == 0)
        return chip(xs[step], y) if along_x else chip(x, ys[step])

    def send(h, p, s, axis, step, part):
        ref = unit(h, p, s, c)
        if part is not None:
            ref = ref.at[part]
        to_p, to_s = ((p - step) % 4, s) if axis == 0 else (p, (s - step) % 4)
        go = copy(
            ref, ref, g_send.at[h, p, s, 2 * axis + (step == 3)], g_recv.at[h, to_p, to_s, part or 0],
            neighbour(h, axis, step),
        )
        go.start()
        waits.append(go)

    def arrive(h, p, s):
        ref = unit(h, p, s, c)
        parts = (0, 1) if (s == 2 or (s == 0 and p == 2)) else (None,)
        for part in parts:
            got = ref if part is None else ref.at[part]
            copy(got, got, g_send.at[h, p, s, 0], g_recv.at[h, p, s, part or 0], partner).wait_recv()

    def relay(h, p, s):
        if s == 0:
            if p == 0:
                send(h, p, s, 0, 1, None)
                send(h, p, s, 0, 3, None)
            elif p == 1:
                send(h, p, s, 0, 3, 1)
            elif p == 3:
                send(h, p, s, 0, 1, 0)
            send(h, p, s, 1, 1, None)
            send(h, p, s, 1, 3, None)
        elif s == 1:
            send(h, p, s, 1, 3, 1)
        elif s == 3:
            send(h, p, s, 1, 1, 0)
        ref = unit(h, p, s, c)
        go = copy(ref, ref, c_send.at[h, p, s], c_recv.at[h, p, s], partner)
        go.start()
        waits.append(go)

    def from_partner(h, p, s):
        ref = unit(h, p, s, 1 - c)
        copy(ref, ref, c_send.at[h, p, s], c_recv.at[h, p, s], partner).wait_recv()

    early, late = jnp.minimum(b, mirror), jnp.maximum(b, mirror)
    job_block = (b, mirror)

    def q_tile(job, j):
        two = qd[job, pl.ds(2 * j, 2)].reshape(2 * ROWS, 2 * D)
        return jnp.concatenate([two[:, :D], two[:, D:]], axis=0)

    def tile_rows(job, j):
        return pl.ds(pl.multiple_of(job * 1024 + j * 256, 256), 256)

    def chunk(pair, half, t):
        return kv[pl.ds(2 * pair, 2), half, :, t].reshape(1024, D)

    def visible(block, j, pair, half, keys):
        at = lax.broadcasted_iota(jnp.int32, (1, keys), 1)
        tile = at >> 6
        k_pos = pair * 2048 + tile * 128 + half * ROWS + (at & 63)
        k_seg = jnp.zeros((1, keys), jnp.int32)
        for n in range(keys // ROWS):
            k_seg = jnp.where(tile == n, seg_ref[pair * 16 + n], k_seg)
        row = lax.broadcasted_iota(jnp.int32, (2 * ROWS, 1), 0)
        q_pos = block * 1024 + (2 * j + (row >> 6)) * 128 + xh * ROWS + (row & 63)
        q_seg = jnp.where(row < ROWS, seg_ref[block * 8 + 2 * j], seg_ref[block * 8 + 2 * j + 1])
        q_seg = jnp.where(q_seg % 2 == 1, q_seg, -1)
        one = (k_pos <= q_pos) | (k_seg == q_seg)
        return jnp.concatenate([one, one], axis=0)

    def full(jobs, pair, half):
        k, v = chunk(pair, half, 0), chunk(pair, half, 1)
        for job in jobs:
            for j in range(4):
                attend(q_tile(job, j), k, v, None, tile_rows(job, j), m_ref, l_ref, acc_ref)

    def masked(job, block, pair, half, keys):
        if keys == 1024:
            k, v = chunk(pair, half, 0), chunk(pair, half, 1)
        else:
            k, v = (kv[2 * pair, half, :, t].reshape(512, D) for t in range(2))
        for j in range(4):
            mask = visible(block, j, pair, half, keys)
            attend(q_tile(job, j), k, v, mask, tile_rows(job, j), m_ref, l_ref, acc_ref)

    def pick(values, i):
        out = jnp.int32(values[0])
        for n in range(1, len(values)):
            out = jnp.where(i == n, jnp.int32(values[n]), out)
        return out

    def compute(offsets):
        def one_chip(i, carry):
            xx = (x + pick([o[0] for o in offsets], i)) % 4
            yy = (y + pick([o[1] for o in offsets], i)) % 4
            pair, half = 2 * yy + xx % 2, xx // 2

            @pl.when(pair < early // 2)
            def _():
                full((0, 1), pair, half)

            @pl.when(pair >= early // 2)
            def _():
                def one_job(job, inner):
                    block = jnp.where(job == 0, job_block[0], job_block[1])

                    @pl.when(pair < block // 2)
                    def _():
                        full((job,), pair, half)

                    @pl.when(pair == block // 2)
                    def _():
                        masked(job, block, pair, half, 1024)

                    @pl.when((pair > block // 2) & (pair == (block + 1) // 2))
                    def _():
                        masked(job, block, pair, half, 512)

                    return inner

                lax.fori_loop(0, 2, one_job, 0)

            return carry

        lax.fori_loop(0, len(offsets), one_chip, 0)

    for h in range(2):
        relay(h, 0, 0)
    first = True
    stages = (
        ((1, 0), (3, 0), (0, 1), (0, 3)),
        ((2, 0), (1, 1), (1, 3), (3, 1), (3, 3), (0, 2)),
        ((2, 1), (2, 3), (1, 2), (3, 2)),
        ((2, 2),),
    )
    for number, stage in enumerate(stages):
        for p, s in stage:
            for h in range(2):
                arrive(h, p, s)
                relay(h, p, s)
        if number == 0:
            q_own.wait()
            for d in order + (0,):
                for job in range(2):
                    if job == 0 and d == 0:
                        continue
                    copy(
                        columns(q_hbm, z * 4 * D, 2 * D), qd.at[job, back[d]],
                        q_send.at[job, d], q_recv.at[job, d], partner,
                    ).wait_recv()
            for h in range(2):
                from_partner(h, 0, 0)
        for p, s in stage:
            for h in range(2):
                from_partner(h, p, s)
        if number < 2:
            compute(ROUNDS[number])
        elif number == 3:
            compute(ROUNDS[2])

    for job in range(2):
        for j in range(4):
            rows = tile_rows(job, j)
            o = (acc_ref[rows, :] / l_ref[rows, :]).astype(jnp.bfloat16)
            o = jnp.concatenate([o[: 2 * ROWS], o[2 * ROWS :]], axis=1)
            od[job, pl.ds(2 * j, 2)] = o.reshape(2, ROWS, 2 * D)
    for d in order + (0,):
        for job in range(2):
            if job == 0 and d == 0:
                continue
            go = copy(
                od.at[job, plane[d]], columns(out_hbm, z * 4 * D + job * 2 * D, 2 * D),
                o_send.at[job, d], o_recv.at[job, d], (2 * plane[d] + xh, mirror if job else b),
            )
            go.start()
            waits.append(go)
    o_own = pltpu.make_async_copy(od.at[0, z], columns(out_hbm, z * 4 * D, 2 * D), here.at[3])
    o_own.start()
    o_own.wait()
    for d in order + (0,):
        for job in range(2):
            if job == 0 and d == 0:
                continue
            copy(
                od.at[job, z], columns(out_hbm, back[d] * 4 * D + job * 2 * D, 2 * D),
                o_send.at[job, d], o_recv.at[job, d], partner,
            ).wait_recv()
    for go in waits:
        go.wait_send()


def local(queries, key_rows, value_rows, tile_segment):
    dma = pltpu.SemaphoreType.DMA
    hbm = pl.BlockSpec(memory_space=pl.ANY)
    out = pl.pallas_call(
        kernel,
        out_shape=jax.ShapeDtypeStruct(queries.shape[1:], jnp.bfloat16),
        in_specs=[pl.BlockSpec(memory_space=pltpu.SMEM), hbm, hbm, hbm],
        out_specs=hbm,
        scratch_shapes=[
            pltpu.VMEM((16, 2, 2, 2, 256, D), jnp.bfloat16),
            pltpu.VMEM((2, 8, ROWS, 2 * D), jnp.bfloat16),
            pltpu.VMEM((2, 8, ROWS, 2 * D), jnp.bfloat16),
            pltpu.VMEM((2048, D), jnp.float32),
            pltpu.VMEM((2048, D), jnp.float32),
            pltpu.VMEM((2048, D), jnp.float32),
            dma((2, 8)), dma((2, 8)),
            dma((2, 8)), dma((2, 8)),
            dma((2, 4, 4, 4)), dma((2, 4, 4, 2)),
            dma((2, 4, 4)), dma((2, 4, 4)),
            dma((2, 8)), dma((2, 8)),
            dma((4,)),
        ],
        compiler_params=pltpu.CompilerParams(
            collective_id=0, has_side_effects=True, vmem_limit_bytes=60 * 2**20
        ),
        name="attention",
    )(tile_segment, queries[0], key_rows[0], value_rows[0])
    return out[None]


def solution(mesh):
    return jax.shard_map(
        local,
        mesh=mesh,
        in_specs=(P("blk", "ulysses", None), P("blk", "ulysses", None), P("blk", "ulysses", None), P()),
        out_specs=P("blk", "ulysses", None),
        check_vma=False,
    )
```

time: 430 us -> 107 us (0.25)
  Pallas kernels: 0 us -> 103 us
  other arithmetic: 98.7 us -> 0 us
  local copies, waits for them, and re-layouts: 73.2 us -> 1.87 us
  blocking collectives: 71.1 us -> 0 us
  loops' own time: 63.6 us -> 0 us
  matrix products: 49.4 us -> 0 us
  waiting for transfers between devices: 42.1 us -> 0 us
  between operations: 13.8 us -> 0.01 us
  starting transfers between devices: 12.9 us -> 0 us
    pallas_call x0 -> x1, Pallas kernels: none -> 103 us  [local(): pl.pallas_call(kernel, out_shape=jax.ShapeDtypeStruct(queries.shape[1:],...]
    all_to_all x3 -> x0, blocking collectives: 71.1 us -> none  [the longest x1 27.8 us: side_by_side(): lax.all_to_all(both, axis, split_axis=split_dim, concat_axis=concat_dim,...]
    another operation x65 -> x0, loops' own time: 63.6 us -> none  [the longest x1 61.4 us: fold_step(): lax.scan(one_block, running, (key_blocks, value_blocks, jnp.arange(block_...]
    dot_general x66 -> x0, matrix products: 49.4 us -> none  [the longest x33 31.2 us: update(): jnp.einsum('kgqs,skd->kgqd', weights.astype(jnp.bfloat16), value_block, p...]
    ppermute x8 -> x0, waiting for transfers between devices: 42.1 us -> none  [partner_2(): lax.ppermute(value, axis, [(i, i ^ 1 << bit) for i in range(lax.axis_size...]
    reduce_or x32 -> x0, other arithmetic: 41.9 us -> none  [one_block(): jnp.any(allowed)]
    squeeze x32 -> x0, local copies, waits for them, and re-layouts: 31.8 us -> none  [fold_step(): lax.scan(one_block, running, (key_blocks, value_blocks, jnp.arange(block_...]
    reduce_sum x66 -> x0, other arithmetic: 26.8 us -> none  [the longest x33 19 us: update(): denominators = factor * denominators + jnp.sum(weights, axis=3)]
  transfers between devices with their start and end apart: 9 -> 0, of which waited for: 8 -> 0; matrix products, arithmetic and copies ran while one was open for 7% -> 0% of each run, Pallas kernels for 0% -> 0%
where the time goes in v1:
time: 107 us; the launch traced here: 105 us
  Pallas kernels  103 us (96%)
  local copies, waits for them, and re-layouts  1.87 us (2%)
    pallas_call x1, Pallas kernels, local(): pl.pallas_call(kernel, out_shape=jax.ShapeDtypeStruct(queries.shape[1:],...  103 us

profile of v1, /device:TPU:17, one launch (start us, length us, event | category | flops | bytes accessed | tf_op | source)
XLA Modules:
  0.0 105.0 jit_solution(2615972547661004268)
XLA Ops:
  0.0 103.1 %attention.1 = bf16[64,4096]{1,0:T(8,128)(2,1)} custom-call(s32[128]{0:T(128)} %seg_ref.1, bf16[64,4096]{1,0:T(8,128)(2,1)} %bitcast.5, bf16[64,1024]{1,0:T(8,128)(2,1)} %bitcast.6, bf16[64,1024]{1,0:T(8,128)(2,1)} %bitcast.7), custom_call_target="tpu_custom_call" | custom-call | tf_op jit(solution)/shard_map/attention/pallas_call | solution.py:320
  103.1 1.9 %copy.6 = bf16[1,64,4096]{2,1,0:T(8,128)(2,1)} copy(bf16[1,64,4096]{2,1,0:T(8,128)(2,1)} %bitcast.4) | data formatting | bytes 1048576

commit v2 on v1

v2 whole, which is shorter than its diff:
```python
import math

import jax
import jax.numpy as jnp
from jax import lax
from jax.experimental import pallas as pl
from jax.experimental.pallas import tpu as pltpu
from jax.sharding import PartitionSpec as P

MESH = pl.DeviceIdType.MESH
D = 128
SCALE = D**-0.5 * math.log2(math.e)
MASKED = -1e30
ROWS = 64
PAIRS = ((1, 0), (0, 0), (1, 1), (1, 3), (0, 1), (0, 3), (1, 2), (0, 2))
STAGES = (
    ((1, 0), (3, 0), (0, 1), (0, 3)),
    ((2, 0), (1, 1), (1, 3), (3, 1), (3, 3), (0, 2)),
    ((2, 1), (2, 3), (1, 2), (3, 2)),
    ((2, 2),),
)


def dot(a, b, contract):
    return lax.dot_general(a, b, ((contract[0], contract[1]), ((), ())), preferred_element_type=jnp.float32)


def attend(tiles, k, v, m_ref, l_ref, acc_ref):
    both = jnp.concatenate([v, jnp.ones_like(v)], axis=1)
    scores = [dot(q, k, ((1,), (1,))) for q, _, _ in tiles]
    weights = []
    for s, (_, rows, mask) in zip(scores, tiles):
        if mask is not None:
            s = jnp.where(mask(), s, MASKED)
        m_old = m_ref[rows, :]
        peak = jnp.max(s, axis=1, keepdims=True) * SCALE
        m_new = jnp.maximum(m_old, jnp.broadcast_to(peak, m_old.shape))
        weights.append((jnp.exp2(s * SCALE - m_new[:, :1]).astype(jnp.bfloat16), jnp.exp2(m_old - m_new)))
        m_ref[rows, :] = m_new
    for (p, alpha), (_, rows, _) in zip(weights, tiles):
        o = dot(p, both, ((1,), (0,)))
        acc_ref[rows, :] = acc_ref[rows, :] * alpha + o[:, :D]
        l_ref[rows, :] = l_ref[rows, :] * alpha + o[:, D:]


def kernel(
    seg_ref, q_hbm, k_hbm, v_hbm, out_hbm,
    kv, qd, od, m_ref, l_ref, acc_ref,
    kv_send, kv_recv, q_send, q_recv, g_send, g_recv, c_send, c_recv, o_send, o_recv, here,
):
    u = lax.axis_index("ulysses")
    b = lax.axis_index("blk")
    z, xh = u // 2, u % 2
    y, xl, c = b // 4, (b // 2) % 2, b % 2
    x = 2 * xh + xl
    mirror = 15 - b

    def chip(xx, yy):
        return (2 * z + xx // 2, 4 * yy + 2 * (xx % 2) + c)

    def copy(src, dst, send, recv, device):
        return pltpu.make_async_remote_copy(
            src_ref=src, dst_ref=dst, send_sem=send, recv_sem=recv, device_id=device, device_id_type=MESH
        )

    plane = [(z + d) % 8 for d in range(8)]
    back = [(z + 8 - d) % 8 for d in range(8)]
    xs = [(x + d) % 4 for d in range(4)]
    ys = [(y + d) % 4 for d in range(4)]
    partner = (u, b + 1 - 2 * c)

    barrier = pltpu.get_barrier_semaphore()
    peers = [(2 * plane[d] + xh, b) for d in range(1, 8)] + [(2 * plane[d] + xh, mirror) for d in range(8)]
    peers += [chip(xs[1], y), chip(xs[3], y), chip(x, ys[1]), chip(x, ys[3]), partner]
    for peer in peers:
        pl.semaphore_signal(barrier, inc=1, device_id=peer, device_id_type=MESH)
    pl.semaphore_wait(barrier, len(peers))

    waits = []

    def kv_group(group, t):
        return kv.at[b, xh, group // 4, t, pl.ds(pl.multiple_of((group % 4) * ROWS, ROWS), ROWS)]

    def columns(ref, start, width):
        return ref.at[:, pl.ds(pl.multiple_of(start, width), width)]

    locals_ = []
    for t, ref in enumerate((k_hbm, v_hbm)):
        own = pltpu.make_async_copy(columns(ref, z * D, D), kv_group(z, t), here.at[t])
        own.start()
        locals_.append(own)
    order = (4, 3, 5, 2, 6, 1, 7)
    for d in order:
        for t, ref in enumerate((k_hbm, v_hbm)):
            go = copy(
                columns(ref, plane[d] * D, D), kv_group(z, t), kv_send.at[t, d], kv_recv.at[t, d],
                (2 * plane[d] + xh, b),
            )
            go.start()
            waits.append(go)
    q_own = pltpu.make_async_copy(columns(q_hbm, z * 4 * D, 2 * D), qd.at[0, z], here.at[2])
    q_own.start()
    for job in range(2):
        for d in order if job == 0 else order + (0,):
            go = copy(
                columns(q_hbm, plane[d] * 4 * D + job * 2 * D, 2 * D), qd.at[job, z],
                q_send.at[job, d], q_recv.at[job, d], (2 * plane[d] + xh, mirror if job else b),
            )
            go.start()
            waits.append(go)

    m_ref[...] = jnp.full(m_ref.shape, MASKED, jnp.float32)
    l_ref[...] = jnp.zeros(l_ref.shape, jnp.float32)
    acc_ref[...] = jnp.zeros(acc_ref.shape, jnp.float32)

    for own in locals_:
        own.wait()
    for d in order:
        for t, ref in enumerate((k_hbm, v_hbm)):
            copy(
                columns(ref, z * D, D), kv_group(back[d], t), kv_send.at[t, d], kv_recv.at[t, d], (u, mirror)
            ).wait_recv()

    def unit(h, p, s, core):
        xx, yy = (xs[p], ys[s]) if h == 0 else (xs[s], ys[p])
        return kv.at[4 * yy + 2 * (xx % 2) + core, xx // 2, h]

    def neighbour(h, axis, step):
        along_x = (axis == 0) == (h == 0)
        return chip(xs[step], y) if along_x else chip(x, ys[step])

    relays = []

    def hop(h, p, s, axis, step, part):
        ref = unit(h, p, s, c)
        if part is not None:
            ref = ref.at[part]
        to_p, to_s = ((p - step) % 4, s) if axis == 0 else (p, (s - step) % 4)
        return copy(
            ref, ref, g_send.at[h, p, s, 2 * axis + (step == 3)], g_recv.at[h, to_p, to_s, part or 0],
            neighbour(h, axis, step),
        )

    def send(*which):
        hop(*which).start()
        relays.append(which)

    def arrive(h, p, s):
        ref = unit(h, p, s, c)
        parts = (0, 1) if (s == 2 or (s == 0 and p == 2)) else (None,)
        for part in parts:
            got = ref if part is None else ref.at[part]
            copy(got, got, g_send.at[h, p, s, 0], g_recv.at[h, p, s, part or 0], partner).wait_recv()

    def relay(h, p, s):
        if s == 0:
            if p == 0:
                send(h, p, s, 0, 1, None)
                send(h, p, s, 0, 3, None)
            elif p == 1:
                send(h, p, s, 0, 3, 1)
            elif p == 3:
                send(h, p, s, 0, 1, 0)
            send(h, p, s, 1, 1, None)
            send(h, p, s, 1, 3, None)
        elif s == 1:
            send(h, p, s, 1, 3, 1)
        elif s == 3:
            send(h, p, s, 1, 1, 0)
        across(h, p, s, c).start()

    def across(h, p, s, core):
        ref = unit(h, p, s, core)
        return copy(ref, ref, c_send.at[h, p, s], c_recv.at[h, p, s], partner)

    def from_partner(h, p, s):
        across(h, p, s, 1 - c).wait_recv()

    early = jnp.where(b < 8, 0, 1)

    def block_of(job):
        return jnp.where(job == 0, b, mirror)

    def q_tile(job, j):
        two = qd[job, pl.ds(2 * j, 2)].reshape(2 * ROWS, 2 * D)
        return jnp.concatenate([two[:, :D], two[:, D:]], axis=0)

    def tile_rows(job, j):
        return pl.ds(pl.multiple_of(job * 1024 + j * 256, 256), 256)

    def masks(block, pair, keys):
        at = lax.broadcasted_iota(jnp.int32, (1, keys), 1)
        tile = ((at >> 10) << 3) + (((at >> 8) & 1) << 2) + ((at >> 6) & 3)
        k_pos = pair * 2048 + tile * 128 + ((at >> 9) & 1) * ROWS + (at & 63)
        k_seg = jnp.zeros((1, keys), jnp.int32)
        for n in range(keys // 128):
            k_seg = jnp.where(tile == n, seg_ref[pair * 16 + n], k_seg)

        def visible(j):
            row = lax.broadcasted_iota(jnp.int32, (2 * ROWS, 1), 0)
            q_pos = block * 1024 + (2 * j + (row >> 6)) * 128 + xh * ROWS + (row & 63)
            q_seg = jnp.where(row < ROWS, seg_ref[block * 8 + 2 * j], seg_ref[block * 8 + 2 * j + 1])
            q_seg = jnp.where(q_seg % 2 == 1, q_seg, -1)
            one = (k_pos <= q_pos) | (k_seg == q_seg)
            return jnp.concatenate([one, one], axis=0)

        return [lambda j=j: visible(j) for j in range(4)]

    def update(job, pair, blocks, mask):
        if blocks == 2:
            k, v = (kv[pl.ds(2 * pair, 2), :, :, t].reshape(2048, D) for t in range(2))
        else:
            k, v = (kv[2 * pair, :, :, t].reshape(1024, D) for t in range(2))
        tiles = [(q_tile(job, j), tile_rows(job, j), mask and mask[j]) for j in range(4)]
        attend(tiles, k, v, m_ref, l_ref, acc_ref)

    def attention(job, i):
        dx, dy = jnp.int32(PAIRS[0][0]), jnp.int32(PAIRS[0][1])
        for n in range(1, 8):
            dx, dy = jnp.where(i == n, PAIRS[n][0], dx), jnp.where(i == n, PAIRS[n][1], dy)
        pair = 2 * ((y + dy) % 4) + (x + dx) % 2
        block = block_of(job)

        @pl.when(pair < block // 2)
        def _():
            update(job, pair, 2, None)

        @pl.when(pair == block // 2)
        def _():
            update(job, pair, 2, masks(block, pair, 2048))

        @pl.when((pair > block // 2) & (pair == (block + 1) // 2))
        def _():
            update(job, pair, 1, masks(block, pair, 1024))

    def giving(job, d):
        return copy(
            od.at[job, plane[d]], columns(out_hbm, z * 4 * D + job * 2 * D, 2 * D),
            o_send.at[job, d], o_recv.at[job, d], (2 * plane[d] + xh, block_of(job)),
        )

    o_own = pltpu.make_async_copy(od.at[0, z], columns(out_hbm, z * 4 * D, 2 * D), here.at[3])

    def give(job):
        for j in range(4):
            rows = tile_rows(job, j)
            o = (acc_ref[rows, :] / l_ref[rows, :]).astype(jnp.bfloat16)
            o = jnp.concatenate([o[: 2 * ROWS], o[2 * ROWS :]], axis=1)
            od[job, pl.ds(2 * j, 2)] = o.reshape(2, ROWS, 2 * D)
        for d in order:
            giving(job, d).start()

        @pl.when(job == 0)
        def _():
            o_own.start()

        @pl.when(job == 1)
        def _():
            giving(job, 0).start()

    def gather(stage):
        for p, s in STAGES[stage]:
            for h in range(2):
                arrive(h, p, s)
                relay(h, p, s)

    def gathered(stage):
        for p, s in STAGES[stage]:
            for h in range(2):
                from_partner(h, p, s)

    def queries_of(job):
        if job == 0:
            q_own.wait()
        for d in order if job == 0 else order + (0,):
            copy(
                columns(q_hbm, z * 4 * D, 2 * D), qd.at[job, back[d]], q_send.at[job, d], q_recv.at[job, d], partner
            ).wait_recv()

    for h in range(2):
        relay(h, 0, 0)
    gather(0)
    queries_of(0)
    for h in range(2):
        from_partner(h, 0, 0)
    gathered(0)

    def step(n, carry):
        @pl.when(n == 1)
        def _():
            queries_of(1)

        @pl.when(n == 2)
        def _():
            gather(1)
            gathered(1)

        @pl.when(n == 5)
        def _():
            gather(2)

        @pl.when(n == 8)
        def _():
            gather(3)
            gathered(2)
            gathered(3)

        @pl.when(n == 12)
        def _():
            give(early)

        job = jnp.where(n < 8, n % 2, jnp.where(n < 12, early, 1 - early))
        attention(job, jnp.where(n < 8, n // 2, 4 + n % 4))
        return carry

    lax.fori_loop(0, 16, step, 0)
    give(1 - early)

    o_own.wait()
    for d in order + (0,):
        for job in range(2):
            if job == 0 and d == 0:
                continue
            copy(
                od.at[job, z], columns(out_hbm, back[d] * 4 * D + job * 2 * D, 2 * D),
                o_send.at[job, d], o_recv.at[job, d], partner,
            ).wait_recv()
            giving(job, d).wait_send()
    for go in waits:
        go.wait_send()
    for which in relays:
        hop(*which).wait_send()
    for stage in (((0, 0),),) + STAGES:
        for p, s in stage:
            for h in range(2):
                across(h, p, s, c).wait_send()


def local(queries, key_rows, value_rows, tile_segment):
    dma = pltpu.SemaphoreType.DMA
    hbm = pl.BlockSpec(memory_space=pl.ANY)
    out = pl.pallas_call(
        kernel,
        out_shape=jax.ShapeDtypeStruct(queries.shape[1:], jnp.bfloat16),
        in_specs=[pl.BlockSpec(memory_space=pltpu.SMEM), hbm, hbm, hbm],
        out_specs=hbm,
        scratch_shapes=[
            pltpu.VMEM((16, 2, 2, 2, 256, D), jnp.bfloat16),
            pltpu.VMEM((2, 8, ROWS, 2 * D), jnp.bfloat16),
            pltpu.VMEM((2, 8, ROWS, 2 * D), jnp.bfloat16),
            pltpu.VMEM((2048, D), jnp.float32),
            pltpu.VMEM((2048, D), jnp.float32),
            pltpu.VMEM((2048, D), jnp.float32),
            dma((2, 8)), dma((2, 8)),
            dma((2, 8)), dma((2, 8)),
            dma((2, 4, 4, 4)), dma((2, 4, 4, 2)),
            dma((2, 4, 4)), dma((2, 4, 4)),
            dma((2, 8)), dma((2, 8)),
            dma((4,)),
        ],
        compiler_params=pltpu.CompilerParams(
            collective_id=0, has_side_effects=True, vmem_limit_bytes=60 * 2**20
        ),
        name="attention",
    )(tile_segment, queries[0], key_rows[0], value_rows[0])
    return out[None]


def solution(mesh):
    return jax.shard_map(
        local,
        mesh=mesh,
        in_specs=(P("blk", "ulysses", None), P("blk", "ulysses", None), P("blk", "ulysses", None), P()),
        out_specs=P("blk", "ulysses", None),
        check_vma=False,
    )
```

time: 107 us -> 82.8 us (0.77); the launches traced: 105 us -> 82.7 us
  Pallas kernels: 103 us -> 80.8 us
    pallas_call x1, Pallas kernels: 103 us -> 80.8 us  [local(): pl.pallas_call(kernel, out_shape=jax.ShapeDtypeStruct(queries.shape[1:],...]
where the time goes in v2:
time: 82.8 us; the launch traced here: 82.7 us
  Pallas kernels  80.8 us (98%)
  local copies, waits for them, and re-layouts  1.87 us (2%)
    pallas_call x1, Pallas kernels, local(): pl.pallas_call(kernel, out_shape=jax.ShapeDtypeStruct(queries.shape[1:],...  80.8 us
    unnamed x1, local copies, waits for them, and re-layouts  1.87 us

profile of v2, /device:TPU:17, one launch (start us, length us, event | category | flops | bytes accessed | tf_op | source)
XLA Modules:
  0.0 82.7 jit_solution(12296652780175411732)
XLA Ops:
  0.0 80.8 %attention.1 = bf16[64,4096]{1,0:T(8,128)(2,1)} custom-call(s32[128]{0:T(128)} %seg_ref.1, bf16[64,4096]{1,0:T(8,128)(2,1)} %bitcast.5, bf16[64,1024]{1,0:T(8,128)(2,1)} %bitcast.6, bf16[64,1024]{1,0:T(8,128)(2,1)} %bitcast.7), custom_call_target="tpu_custom_call" | custom-call | tf_op jit(solution)/shard_map/attention/pallas_call | solution.py:342
  80.8 1.9 %copy.6 = bf16[1,64,4096]{2,1,0:T(8,128)(2,1)} copy(bf16[1,64,4096]{2,1,0:T(8,128)(2,1)} %bitcast.4) | data formatting | bytes 1048576

commit v3 on v2

--- a/solution.py
+++ b/solution.py
@@ -44,8 +44,8 @@
 
 
 def kernel(
-    seg_ref, q_hbm, k_hbm, v_hbm, out_hbm,
-    kv, qd, od, m_ref, l_ref, acc_ref,
+    seg_ref, q_in, k_in, v_in, out_hbm,
+    q_hbm, k_hbm, v_hbm, kv, qd, od, m_ref, l_ref, acc_ref,
     kv_send, kv_recv, q_send, q_recv, g_send, g_recv, c_send, c_recv, o_send, o_recv, here,
 ):
     u = lax.axis_index("ulysses")
@@ -74,6 +74,11 @@
     peers += [chip(xs[1], y), chip(xs[3], y), chip(x, ys[1]), chip(x, ys[3]), partner]
     for peer in peers:
         pl.semaphore_signal(barrier, inc=1, device_id=peer, device_id_type=MESH)
+    staged = []
+    for n, (src, dst) in enumerate(((k_in, k_hbm), (v_in, v_hbm), (q_in, q_hbm))):
+        stage = pltpu.make_async_copy(src, dst, here.at[n])
+        stage.start()
+        staged.append(stage)
     pl.semaphore_wait(barrier, len(peers))
 
     waits = []
@@ -84,21 +89,23 @@
     def columns(ref, start, width):
         return ref.at[:, pl.ds(pl.multiple_of(start, width), width)]
 
+    for stage in staged:
+        stage.wait()
     locals_ = []
-    for t, ref in enumerate((k_hbm, v_hbm)):
+    for t, ref in enumerate((k_in, v_in)):
         own = pltpu.make_async_copy(columns(ref, z * D, D), kv_group(z, t), here.at[t])
         own.start()
         locals_.append(own)
     order = (4, 3, 5, 2, 6, 1, 7)
-    for d in order:
-        for t, ref in enumerate((k_hbm, v_hbm)):
+    for t, ref in enumerate((k_hbm, v_hbm)):
+        for d in order:
             go = copy(
                 columns(ref, plane[d] * D, D), kv_group(z, t), kv_send.at[t, d], kv_recv.at[t, d],
                 (2 * plane[d] + xh, b),
             )
             go.start()
             waits.append(go)
-    q_own = pltpu.make_async_copy(columns(q_hbm, z * 4 * D, 2 * D), qd.at[0, z], here.at[2])
+    q_own = pltpu.make_async_copy(columns(q_in, z * 4 * D, 2 * D), qd.at[0, z], here.at[2])
     q_own.start()
     for job in range(2):
         for d in order if job == 0 else order + (0,):
@@ -113,14 +120,6 @@
     l_ref[...] = jnp.zeros(l_ref.shape, jnp.float32)
     acc_ref[...] = jnp.zeros(acc_ref.shape, jnp.float32)
 
-    for own in locals_:
-        own.wait()
-    for d in order:
-        for t, ref in enumerate((k_hbm, v_hbm)):
-            copy(
-                columns(ref, z * D, D), kv_group(back[d], t), kv_send.at[t, d], kv_recv.at[t, d], (u, mirror)
-            ).wait_recv()
-
     def unit(h, p, s, core):
         xx, yy = (xs[p], ys[s]) if h == 0 else (xs[s], ys[p])
         return kv.at[4 * yy + 2 * (xx % 2) + core, xx // 2, h]
@@ -129,52 +128,66 @@
         along_x = (axis == 0) == (h == 0)
         return chip(xs[step], y) if along_x else chip(x, ys[step])
 
-    relays = []
-
-    def hop(h, p, s, axis, step, part):
-        ref = unit(h, p, s, c)
-        if part is not None:
-            ref = ref.at[part]
+    def wanted(h, p, s, core, y_to):
+        x_from, y_from = (xs[p], ys[s]) if h == 0 else (xs[s], ys[p])
+        return (y_from != 3) | (y_to == 0) | (y_to == 3) | ((core == 0) & (x_from % 2 == 0))
+
+    def is_along_x(h, axis):
+        return (axis == 0) == (h == 0)
+
+    def hop(h, p, s, t, axis, step):
+        ref = unit(h, p, s, c).at[t]
         to_p, to_s = ((p - step) % 4, s) if axis == 0 else (p, (s - step) % 4)
         return copy(
-            ref, ref, g_send.at[h, p, s, 2 * axis + (step == 3)], g_recv.at[h, to_p, to_s, part or 0],
+            ref, ref, g_send.at[h, p, s, 2 * axis + (step == 3), t], g_recv.at[h, to_p, to_s, t],
             neighbour(h, axis, step),
         )
 
-    def send(*which):
-        hop(*which).start()
-        relays.append(which)
-
-    def arrive(h, p, s):
-        ref = unit(h, p, s, c)
-        parts = (0, 1) if (s == 2 or (s == 0 and p == 2)) else (None,)
-        for part in parts:
-            got = ref if part is None else ref.at[part]
-            copy(got, got, g_send.at[h, p, s, 0], g_recv.at[h, p, s, part or 0], partner).wait_recv()
-
-    def relay(h, p, s):
-        if s == 0:
-            if p == 0:
-                send(h, p, s, 0, 1, None)
-                send(h, p, s, 0, 3, None)
-            elif p == 1:
-                send(h, p, s, 0, 3, 1)
-            elif p == 3:
-                send(h, p, s, 0, 1, 0)
-            send(h, p, s, 1, 1, None)
-            send(h, p, s, 1, 3, None)
-        elif s == 1:
-            send(h, p, s, 1, 3, 1)
-        elif s == 3:
-            send(h, p, s, 1, 1, 0)
-        across(h, p, s, c).start()
-
-    def across(h, p, s, core):
-        ref = unit(h, p, s, core)
-        return copy(ref, ref, c_send.at[h, p, s], c_recv.at[h, p, s], partner)
+    def goes(h, p, s, t, axis, step):
+        along_x = is_along_x(h, axis)
+        y_to = y if along_x else ys[step]
+        yes = wanted(h, p, s, c, y) & wanted(h, p, s, c, y_to)
+        at = p if axis == 0 else s
+        if at and not along_x:
+            turned = (ys[at] == 0) & (y_to == 2)
+            if at == 3:
+                yes = yes & jnp.logical_not(turned)
+            elif t == 0:
+                yes = yes & turned
+        return yes
+
+    def hops(h, p, s, t):
+        found = []
+        for axis in (0, 1) if s == 0 else (1,):
+            at = p if axis == 0 else s
+            if at in (0, 3) and (at == 0 or t == 0):
+                found.append((h, p, s, t, axis, 1))
+            if at == 0 or (at == 1 and (t == 1 or not is_along_x(h, axis))):
+                found.append((h, p, s, t, axis, 3))
+        return found
+
+    def relay(h, p, s, t):
+        for which in hops(h, p, s, t):
+
+            @pl.when(goes(*which))
+            def _():
+                hop(*which).start()
+
+        across(h, p, s, t, c).start()
+
+    def arrive(h, p, s, t):
+        ref = unit(h, p, s, c).at[t]
+        copy(ref, ref, g_send.at[h, p, s, 0, t], g_recv.at[h, p, s, t], partner).wait_recv()
+
+    def across(h, p, s, t, core):
+        ref = unit(h, p, s, core).at[t]
+        return copy(ref, ref, c_send.at[h, p, s, t], c_recv.at[h, p, s, t], partner)
 
     def from_partner(h, p, s):
-        across(h, p, s, 1 - c).wait_recv()
+        @pl.when(wanted(h, p, s, 1 - c, y))
+        def _():
+            for t in range(2):
+                across(h, p, s, t, 1 - c).wait_recv()
 
     early = jnp.where(b < 8, 0, 1)
 
@@ -192,16 +205,18 @@
         at = lax.broadcasted_iota(jnp.int32, (1, keys), 1)
         tile = ((at >> 10) << 3) + (((at >> 8) & 1) << 2) + ((at >> 6) & 3)
         k_pos = pair * 2048 + tile * 128 + ((at >> 9) & 1) * ROWS + (at & 63)
-        k_seg = jnp.zeros((1, keys), jnp.int32)
-        for n in range(keys // 128):
-            k_seg = jnp.where(tile == n, seg_ref[pair * 16 + n], k_seg)
+        first = pair * 16
+        start, image = jnp.maximum(first - 8, 0), jnp.full((1, keys), 1 << 20, jnp.int32)
+        for n in range(-7, keys // 128):
+            at_tile = jnp.maximum(first + n, 0)
+            start = jnp.where(seg_ref[at_tile] == seg_ref[jnp.maximum(first + n - 1, 0)], start, at_tile)
+            if n >= 0:
+                image = jnp.where(tile == n, jnp.where(seg_ref[at_tile] % 2 == 1, start * 128, 1 << 20), image)
+        k_from = jnp.minimum(k_pos, image)
 
         def visible(j):
             row = lax.broadcasted_iota(jnp.int32, (2 * ROWS, 1), 0)
-            q_pos = block * 1024 + (2 * j + (row >> 6)) * 128 + xh * ROWS + (row & 63)
-            q_seg = jnp.where(row < ROWS, seg_ref[block * 8 + 2 * j], seg_ref[block * 8 + 2 * j + 1])
-            q_seg = jnp.where(q_seg % 2 == 1, q_seg, -1)
-            one = (k_pos <= q_pos) | (k_seg == q_seg)
+            one = k_from <= block * 1024 + (2 * j + (row >> 6)) * 128 + xh * ROWS + (row & 63)
             return jnp.concatenate([one, one], axis=0)
 
         return [lambda j=j: visible(j) for j in range(4)]
@@ -259,10 +274,14 @@
             giving(job, 0).start()
 
     def gather(stage):
-        for p, s in STAGES[stage]:
-            for h in range(2):
-                arrive(h, p, s)
-                relay(h, p, s)
+        for t in range(2):
+            for p, s in STAGES[stage]:
+                for h in range(2):
+
+                    @pl.when(wanted(h, p, s, c, y))
+                    def _():
+                        arrive(h, p, s, t)
+                        relay(h, p, s, t)
 
     def gathered(stage):
         for p, s in STAGES[stage]:
@@ -277,8 +296,14 @@
                 columns(q_hbm, z * 4 * D, 2 * D), qd.at[job, back[d]], q_send.at[job, d], q_recv.at[job, d], partner
             ).wait_recv()
 
-    for h in range(2):
-        relay(h, 0, 0)
+    for t, ref in enumerate((k_hbm, v_hbm)):
+        locals_[t].wait()
+        for d in order:
+            copy(
+                columns(ref, z * D, D), kv_group(back[d], t), kv_send.at[t, d], kv_recv.at[t, d], (u, mirror)
+            ).wait_recv()
+        for h in range(2):
+            relay(h, 0, 0, t)
     gather(0)
     queries_of(0)
     for h in range(2):
@@ -315,6 +340,22 @@
 
     lax.fori_loop(0, 16, step, 0)
     give(1 - early)
+
+    for go in waits:
+        go.wait_send()
+    for stage in (((0, 0),),) + STAGES:
+        for p, s in stage:
+            for h in range(2):
+
+                @pl.when(wanted(h, p, s, c, y))
+                def _():
+                    for t in range(2):
+                        across(h, p, s, t, c).wait_send()
+                        for which in hops(h, p, s, t):
+
+                            @pl.when(goes(*which))
+                            def _():
+                                hop(*which).wait_send()
 
     o_own.wait()
     for d in order + (0,):
@@ -326,14 +367,6 @@
                 o_send.at[job, d], o_recv.at[job, d], partner,
             ).wait_recv()
             giving(job, d).wait_send()
-    for go in waits:
-        go.wait_send()
-    for which in relays:
-        hop(*which).wait_send()
-    for stage in (((0, 0),),) + STAGES:
-        for p, s in stage:
-            for h in range(2):
-                across(h, p, s, c).wait_send()
 
 
 def local(queries, key_rows, value_rows, tile_segment):
@@ -345,6 +378,9 @@
         in_specs=[pl.BlockSpec(memory_space=pltpu.SMEM), hbm, hbm, hbm],
         out_specs=hbm,
         scratch_shapes=[
+            pltpu.VMEM(queries.shape[1:], jnp.bfloat16),
+            pltpu.VMEM(key_rows.shape[1:], jnp.bfloat16),
+            pltpu.VMEM(value_rows.shape[1:], jnp.bfloat16),
             pltpu.VMEM((16, 2, 2, 2, 256, D), jnp.bfloat16),
             pltpu.VMEM((2, 8, ROWS, 2 * D), jnp.bfloat16),
             pltpu.VMEM((2, 8, ROWS, 2 * D), jnp.bfloat16),
@@ -353,8 +389,8 @@
             pltpu.VMEM((2048, D), jnp.float32),
             dma((2, 8)), dma((2, 8)),
             dma((2, 8)), dma((2, 8)),
-            dma((2, 4, 4, 4)), dma((2, 4, 4, 2)),
-            dma((2, 4, 4)), dma((2, 4, 4)),
+            dma((2, 4, 4, 4, 2)), dma((2, 4, 4, 2)),
+            dma((2, 4, 4, 2)), dma((2, 4, 4, 2)),
             dma((2, 8)), dma((2, 8)),
             dma((4,)),
         ],

time: 82.8 us -> 81.2 us (0.981)
  Pallas kernels: 80.8 us -> 78.4 us
    pallas_call x1, Pallas kernels: 80.8 us -> 78.4 us  [local(): pl.pallas_call(kernel, out_shape=jax.ShapeDtypeStruct(queries.shape[1:],...]
where the time goes in v3:
time: 81.2 us; the launch traced here: 80.2 us
  Pallas kernels  78.4 us (97%)
  local copies, waits for them, and re-layouts  1.87 us (2%)
    pallas_call x1, Pallas kernels, local(): pl.pallas_call(kernel, out_shape=jax.ShapeDtypeStruct(queries.shape[1:],...  78.4 us
    unnamed x1, local copies, waits for them, and re-layouts  1.87 us

profile of v3, /device:TPU:17, one launch (start us, length us, event | category | flops | bytes accessed | tf_op | source)
XLA Modules:
  0.0 80.2 jit_solution(17440414832327952235)
XLA Ops:
  0.0 78.4 %attention.1 = bf16[64,4096]{1,0:T(8,128)(2,1)} custom-call(s32[128]{0:T(128)} %seg_ref.1, bf16[64,4096]{1,0:T(8,128)(2,1)} %bitcast.5, bf16[64,1024]{1,0:T(8,128)(2,1)} %bitcast.6, bf16[64,1024]{1,0:T(8,128)(2,1)} %bitcast.7), custom_call_target="tpu_custom_call" | custom-call | tf_op jit(solution)/shard_map/attention/pallas_call | solution.py:375
  78.4 1.9 %copy.6 = bf16[1,64,4096]{2,1,0:T(8,128)(2,1)} copy(bf16[1,64,4096]{2,1,0:T(8,128)(2,1)} %bitcast.4) | data formatting | bytes 1048576
